TPU v7x, 8 devices: a whole 2x2x1 slice. The times are simulated.
8 devices in a mesh: dp: 2 (over z, y), stage: 4 (over x, core).
Axes of the slice: x: 2, y: 2, z: 1, core: 2. Of those that a mesh axis runs over, the one named last changes fastest.
Arguments:
- tokens_in: bfloat16 [32, 1024, 768], P('dp'), parts along dimension 0
- targets: bfloat16 [32, 1024, 768], P('dp'), parts along dimension 0
- w_in: bfloat16 [8, 768, 3072], P('stage')
- w_out: bfloat16 [8, 3072, 768], P('stage')
- norm_gains: float32 [8, 768], P('stage')
Outputs:
- output 1: float32 [16, 768, 3072], P(('dp', 'stage')), parts along dimension 0
- output 2: float32 [16, 3072, 768], P(('dp', 'stage')), parts along dimension 0
- output 3: float32 [16, 768], P(('dp', 'stage')), parts along dimension 0
- output 4: float32 [2], P('dp'), parts along dimension 0
There are 2 independent parts. A program takes and returns all parts, laid end to end along the dimension named above; an argument that names none is the same for every part.
All inputs are finite; a program needn't handle non-finite values.
Results may differ from a plain program's by a relative error of at most 0.00215886.
Values are sent between devices in bfloat16 or wider.
A program may use at most 1 GiB of HBM per device.

v0:
```python
import jax
import jax.numpy as jnp
from jax import lax
from jax.sharding import PartitionSpec as P

EPSILON = 1e-6


def norm_scale(x_f32, gain_vec):
    inv_rms = lax.rsqrt(jnp.mean(x_f32 * x_f32, axis=-1, keepdims=True) + EPSILON)
    return x_f32 * inv_rms * gain_vec


def layer_forward(x_act, first_w, second_w, gain_vec):
    x_f32 = x_act.astype(jnp.float32)
    normed = norm_scale(x_f32, gain_vec).astype(jnp.bfloat16)
    pre_act = jnp.dot(normed, first_w, preferred_element_type=jnp.float32)
    hidden = jax.nn.gelu(pre_act).astype(jnp.bfloat16)
    out_f32 = jnp.dot(hidden, second_w, preferred_element_type=jnp.float32)
    return (x_f32 + out_f32).astype(jnp.bfloat16)


def layer_backward(x_act, grad_h, first_w, second_w, gain_vec):
    x_f32 = x_act.astype(jnp.float32)
    normed_f32, norm_vjp = jax.vjp(norm_scale, x_f32, gain_vec)
    normed = normed_f32.astype(jnp.bfloat16)
    pre_act = jnp.dot(normed, first_w, preferred_element_type=jnp.float32)
    hidden_f32, gelu_vjp = jax.vjp(jax.nn.gelu, pre_act)
    hidden = hidden_f32.astype(jnp.bfloat16)
    grad_second = jnp.einsum('tf,td->fd', hidden, grad_h, preferred_element_type=jnp.float32)
    grad_hidden = jnp.einsum('td,fd->tf', grad_h, second_w, preferred_element_type=jnp.float32)
    grad_pre = gelu_vjp(grad_hidden)[0].astype(jnp.bfloat16)
    grad_first = jnp.einsum('td,tf->df', normed, grad_pre, preferred_element_type=jnp.float32)
    grad_normed = jnp.einsum('tf,df->td', grad_pre, first_w, preferred_element_type=jnp.float32)
    grad_x_norm, grad_gain = norm_vjp(grad_normed)
    grad_x = (grad_h.astype(jnp.float32) + grad_x_norm).astype(jnp.bfloat16)
    return grad_x, grad_first, grad_second, grad_gain


def segment_forward(x_act, first_w, second_w, gain_rows):
    kept_list = []
    for layer_idx in range(first_w.shape[0]):
        kept_list.append(x_act)
        x_act = layer_forward(x_act, first_w[layer_idx], second_w[layer_idx], gain_rows[layer_idx])
    return x_act, jnp.stack(kept_list)


def segment_backward(kept_inputs, grad_h, first_w, second_w, gain_rows, grad_sums):
    layer_count = first_w.shape[0]
    first_list = [None] * layer_count
    second_list = [None] * layer_count
    gain_list = [None] * layer_count
    for layer_idx in reversed(range(layer_count)):
        grad_h, grad_first, grad_second, grad_gain = layer_backward(
            kept_inputs[layer_idx], grad_h, first_w[layer_idx], second_w[layer_idx], gain_rows[layer_idx])
        first_list[layer_idx] = grad_first
        second_list[layer_idx] = grad_second
        gain_list[layer_idx] = grad_gain
    new_sums = (grad_sums[0] + jnp.stack(first_list), grad_sums[1] + jnp.stack(second_list),
                grad_sums[2] + jnp.stack(gain_list))
    return grad_h, new_sums


def store_inputs(buffer_all, kept_inputs, mb_index, is_valid):
    old_rows = lax.dynamic_index_in_dim(buffer_all, mb_index, 1, keepdims=False)
    return lax.dynamic_update_index_in_dim(buffer_all, jnp.where(is_valid, kept_inputs, old_rows), mb_index, 1)


def solution(mesh):
    stages = mesh.shape['stage']
    down_perm = [(src_idx, src_idx + 1) for src_idx in range(stages - 1)]
    up_perm = [(src_idx + 1, src_idx) for src_idx in range(stages - 1)]

    def device_step(tokens, targets, w_in, w_out, norm_gains):
        stage_idx = lax.axis_index('stage')
        micro_count, tokens_mb, d_model = tokens.shape
        d_ff = w_in.shape[2]
        segment = w_in.shape[0] // 2
        tick_count = micro_count + 2 * stages - 1
        is_first = stage_idx == 0
        is_last = stage_idx == stages - 1
        up_offset = 2 * stages - 1 - stage_idx
        down_weights = (w_in[:segment], w_out[:segment], norm_gains[:segment])
        up_weights = (w_in[segment:], w_out[segment:], norm_gains[segment:])
        zero_act = jnp.zeros((tokens_mb, d_model), jnp.bfloat16)
        zero_saved = jnp.zeros((segment,) + tokens.shape, jnp.bfloat16)

        def run_down(x_act):
            return segment_forward(x_act, down_weights[0], down_weights[1], down_weights[2])

        def run_up(x_act):
            return segment_forward(x_act, up_weights[0], up_weights[1], up_weights[2])

        def skip_forward(x_act):
            return x_act, jnp.zeros((segment, tokens_mb, d_model), jnp.bfloat16)

        def forward_tick(loop_state, tick_idx):
            in_down, in_up, saved_down, saved_up, finals = loop_state
            mb_down = tick_idx - stage_idx
            mb_up = tick_idx - up_offset
            ok_down = (mb_down >= 0) & (mb_down < micro_count)
            ok_up = (mb_up >= 0) & (mb_up < micro_count)
            idx_down = jnp.clip(mb_down, 0, micro_count - 1)
            idx_up = jnp.clip(mb_up, 0, micro_count - 1)
            in_down = jnp.where(is_first, lax.dynamic_index_in_dim(tokens, idx_down, 0, keepdims=False), in_down)
            out_down, kept_down = lax.cond(ok_down, run_down, skip_forward, in_down)
            out_up, kept_up = lax.cond(ok_up, run_up, skip_forward, in_up)
            saved_down = store_inputs(saved_down, kept_down, idx_down, ok_down)
            saved_up = store_inputs(saved_up, kept_up, idx_up, ok_up)
            old_final = lax.dynamic_index_in_dim(finals, idx_up, 0, keepdims=False)
            finals = lax.dynamic_update_index_in_dim(
                finals, jnp.where(ok_up & is_first, out_up, old_final), idx_up, 0)
            recv_down = lax.ppermute(out_down, 'stage', down_perm)
            recv_up = lax.ppermute(out_up, 'stage', up_perm)
            next_up = jnp.where(is_last, out_down, recv_up)
            return (recv_down, next_up, saved_down, saved_up, finals), None

        fwd_init = (zero_act, zero_act, zero_saved, zero_saved, jnp.zeros(tokens.shape, jnp.bfloat16))
        fwd_state, _ = lax.scan(forward_tick, fwd_init, jnp.arange(tick_count))
        saved_down, saved_up, finals = fwd_state[2], fwd_state[3], fwd_state[4]
        error_f32 = finals.astype(jnp.float32) - targets.astype(jnp.float32)
        seed_grads = (error_f32 * (2.0 / (micro_count * tokens_mb))).astype(jnp.bfloat16)
        sse_local = jnp.where(is_first, jnp.sum(error_f32 * error_f32), 0.0)
        loss_value = lax.psum(sse_local, 'stage') / (micro_count * tokens_mb * d_model)

        def run_down_back(operand):
            return segment_backward(operand[1], operand[0], down_weights[0], down_weights[1],
                                    down_weights[2], operand[2])

        def run_up_back(operand):
            return segment_backward(operand[1], operand[0], up_weights[0], up_weights[1],
                                    up_weights[2], operand[2])

        def skip_backward(operand):
            return jnp.zeros_like(operand[0]), operand[2]

        def backward_tick(loop_state, tick_idx):
            grad_up_in, grad_down_in, sums_up, sums_down = loop_state
            mb_up = tick_idx - stage_idx
            mb_down = tick_idx - up_offset
            ok_up = (mb_up >= 0) & (mb_up < micro_count)
            ok_down = (mb_down >= 0) & (mb_down < micro_count)
            idx_up = jnp.clip(mb_up, 0, micro_count - 1)
            idx_down = jnp.clip(mb_down, 0, micro_count - 1)
            grad_up_in = jnp.where(is_first, lax.dynamic_index_in_dim(seed_grads, idx_up, 0, keepdims=False),
                                   grad_up_in)
            kept_up = lax.dynamic_index_in_dim(saved_up, idx_up, 1, keepdims=False)
            kept_down = lax.dynamic_index_in_dim(saved_down, idx_down, 1, keepdims=False)
            grad_up_out, sums_up = lax.cond(ok_up, run_up_back, skip_backward, (grad_up_in, kept_up, sums_up))
            grad_down_out, sums_down = lax.cond(ok_down, run_down_back, skip_backward,
                                                (grad_down_in, kept_down, sums_down))
            recv_up = lax.ppermute(grad_up_out, 'stage', down_perm)
            recv_down = lax.ppermute(grad_down_out, 'stage', up_perm)
            next_down = jnp.where(is_last, grad_up_out, recv_down)
            return (recv_up, next_down, sums_up, sums_down), None

        zero_sums = (jnp.zeros((segment, d_model, d_ff), jnp.float32),
                     jnp.zeros((segment, d_ff, d_model), jnp.float32),
                     jnp.zeros((segment, d_model), jnp.float32))
        back_init = (zero_act, zero_act, zero_sums, zero_sums)
        back_state, _ = lax.scan(backward_tick, back_init, jnp.arange(tick_count))
        sums_up, sums_down = back_state[2], back_state[3]
        grad_w_in = jnp.concatenate([sums_down[0], sums_up[0]], axis=0)
        grad_w_out = jnp.concatenate([sums_down[1], sums_up[1]], axis=0)
        grad_gains = jnp.concatenate([sums_down[2], sums_up[2]], axis=0)
        return grad_w_in, grad_w_out, grad_gains, loss_value.reshape(1)

    block_spec = P(('dp', 'stage'))
    return jax.shard_map(device_step, mesh=mesh,
                         in_specs=(P('dp'), P('dp'), P('stage'), P('stage'), P('stage')),
                         out_specs=(block_spec, block_spec, block_spec, P('dp')),
                         check_vma=False)
```

profile of v0, /device:TPU:6, one launch (start us, length us, event | category | flops | bytes accessed | tf_op | source)
XLA Modules:
  0.0 4416.7 jit_solution(17580908151970927369)
XLA Ops:
  40.6 1201.4 %while.47 = (s32[]{:T(128)}, bf16[1024,768]{1,0:T(8,128)(2,1)}, bf16[1024,768]{1,0:T(8,128)(2,1)S(1)}, bf16[1,16,1024,768]{3,2,1,0:T(8,128)(2,1)}, bf16[1,16,102...) while((s32[]{:T(128)}, bf16[1024,768]{1,0:T(8,128)(2,1)}, ...), condition=%wide.region_7.8_spmd.clone, body=%wide.region_0.7_spmd.clone.sunk | while | flops 19404425216 | bytes 77122096 | solution.py:119
  1291.6 3089.4 %while.48 = (s32[]{:T(128)}, bf16[1024,768]{1,0:T(8,128)(2,1)S(1)}, bf16[1024,768]{1,0:T(8,128)(2,1)}, f32[1,768,3072]{2,1,0:T(8,128)}, f32[1,3072,768]{2,1,0:T(...) while((s32[]{:T(128)}, bf16[1024,768]{1,0:T(8,128)(2,1)S(1)}, ...), condition=%wide.region_19.20_spmd.clone, body=%wide.region_8.19_spmd.clone.sunk | while | flops 48556679168 | bytes 424871040 | solution.py:161
  1397.1 77.2 %collective-permute-done.2 = bf16[1024,768]{1,0:T(8,128)(2,1)S(1)} collective-permute-done((bf16[1024,768]{1,0:T(8,128)(2,1)S(1)}, bf16[1024,768]{1,0:T(8,128)(2,1)S(1)}, u32[]{:S(2)}, u32[]{:S(2)}) %collective-permute-start.2) | collective-permute-done | bytes 1572896 | tf_op jit(solution)/shard_map/while/body/eval_jaxpr/ppermute | solution.py:152
  1488.1 66.6 %conditional.14 = (bf16[1024,768]{1,0:T(8,128)(2,1)S(1)}, f32[1,768,3072]{2,1,0:T(8,128)}, f32[1,3072,768]{2,1,0:T(8,128)}, f32[1,768]{1,0:T(1,128)S(1)}) conditional(s32[]{:T(128)} %convert_element_type.320, (f32[1,768,3072]{2,1,0:T(8,128)}, f32[1,3072,768]{2,1,0:T(8,128)}, f32[1,768]{1,0:T(1,128)S(1)}) %tuple.109, (pred[]{:T(512)}, s32[]{:T(128)}, ...), branch_computations={%region_9.9_spmd, %region_10.13_spmd} | conditional | flops 24277159936 | bytes 199846112 | solution.py:149
  1591.0 66.2 %conditional.14 = (bf16[1024,768]{1,0:T(8,128)(2,1)S(1)}, f32[1,768,3072]{2,1,0:T(8,128)}, f32[1,3072,768]{2,1,0:T(8,128)}, f32[1,768]{1,0:T(1,128)S(1)}) conditional(s32[]{:T(128)} %convert_element_type.320, (f32[1,768,3072]{2,1,0:T(8,128)}, f32[1,3072,768]{2,1,0:T(8,128)}, f32[1,768]{1,0:T(1,128)S(1)}) %tuple.109, (pred[]{:T(512)}, s32[]{:T(128)}, ...), branch_computations={%region_9.9_spmd, %region_10.13_spmd} | conditional | flops 24277159936 | bytes 199846112 | solution.py:149
  1693.9 66.0 %conditional.14 = (bf16[1024,768]{1,0:T(8,128)(2,1)S(1)}, f32[1,768,3072]{2,1,0:T(8,128)}, f32[1,3072,768]{2,1,0:T(8,128)}, f32[1,768]{1,0:T(1,128)S(1)}) conditional(s32[]{:T(128)} %convert_element_type.320, (f32[1,768,3072]{2,1,0:T(8,128)}, f32[1,3072,768]{2,1,0:T(8,128)}, f32[1,768]{1,0:T(1,128)S(1)}) %tuple.109, (pred[]{:T(512)}, s32[]{:T(128)}, ...), branch_computations={%region_9.9_spmd, %region_10.13_spmd} | conditional | flops 24277159936 | bytes 199846112 | solution.py:149
  1808.5 66.1 %conditional.15 = (bf16[1024,768]{1,0:T(8,128)(2,1)}, f32[1,768,3072]{2,1,0:T(8,128)}, f32[1,3072,768]{2,1,0:T(8,128)}, f32[1,768]{1,0:T(1,128)S(1)}) conditional(s32[]{:T(128)} %convert_element_type.321, (f32[1,768,3072]{2,1,0:T(8,128)}, f32[1,3072,768]{2,1,0:T(8,128)}, f32[1,768]{1,0:T(1,128)S(1)}) %tuple.111, (s32[]{:T(128)}, ...), branch_computations={%region_14.14_spmd, %region_15.18_spmd.clone} | conditional | flops 24278732800 | bytes 207698176 | solution.py:150
  1877.2 66.3 %conditional.14 = (bf16[1024,768]{1,0:T(8,128)(2,1)S(1)}, f32[1,768,3072]{2,1,0:T(8,128)}, f32[1,3072,768]{2,1,0:T(8,128)}, f32[1,768]{1,0:T(1,128)S(1)}) conditional(s32[]{:T(128)} %convert_element_type.320, (f32[1,768,3072]{2,1,0:T(8,128)}, f32[1,3072,768]{2,1,0:T(8,128)}, f32[1,768]{1,0:T(1,128)S(1)}) %tuple.109, (pred[]{:T(512)}, s32[]{:T(128)}, ...), branch_computations={%region_9.9_spmd, %region_10.13_spmd} | conditional | flops 24277159936 | bytes 199846112 | solution.py:149
  1967.2 65.8 %conditional.15 = (bf16[1024,768]{1,0:T(8,128)(2,1)}, f32[1,768,3072]{2,1,0:T(8,128)}, f32[1,3072,768]{2,1,0:T(8,128)}, f32[1,768]{1,0:T(1,128)S(1)}) conditional(s32[]{:T(128)} %convert_element_type.321, (f32[1,768,3072]{2,1,0:T(8,128)}, f32[1,3072,768]{2,1,0:T(8,128)}, f32[1,768]{1,0:T(1,128)S(1)}) %tuple.111, (s32[]{:T(128)}, ...), branch_computations={%region_14.14_spmd, %region_15.18_spmd.clone} | conditional | flops 24278732800 | bytes 207698176 | solution.py:150
  2035.7 66.6 %conditional.14 = (bf16[1024,768]{1,0:T(8,128)(2,1)S(1)}, f32[1,768,3072]{2,1,0:T(8,128)}, f32[1,3072,768]{2,1,0:T(8,128)}, f32[1,768]{1,0:T(1,128)S(1)}) conditional(s32[]{:T(128)} %convert_element_type.320, (f32[1,768,3072]{2,1,0:T(8,128)}, f32[1,3072,768]{2,1,0:T(8,128)}, f32[1,768]{1,0:T(1,128)S(1)}) %tuple.109, (pred[]{:T(512)}, s32[]{:T(128)}, ...), branch_computations={%region_9.9_spmd, %region_10.13_spmd} | conditional | flops 24277159936 | bytes 199846112 | solution.py:149
  2125.6 66.1 %conditional.15 = (bf16[1024,768]{1,0:T(8,128)(2,1)}, f32[1,768,3072]{2,1,0:T(8,128)}, f32[1,3072,768]{2,1,0:T(8,128)}, f32[1,768]{1,0:T(1,128)S(1)}) conditional(s32[]{:T(128)} %convert_element_type.321, (f32[1,768,3072]{2,1,0:T(8,128)}, f32[1,3072,768]{2,1,0:T(8,128)}, f32[1,768]{1,0:T(1,128)S(1)}) %tuple.111, (s32[]{:T(128)}, ...), branch_computations={%region_14.14_spmd, %region_15.18_spmd.clone} | conditional | flops 24278732800 | bytes 207698176 | solution.py:150
  2194.3 66.0 %conditional.14 = (bf16[1024,768]{1,0:T(8,128)(2,1)S(1)}, f32[1,768,3072]{2,1,0:T(8,128)}, f32[1,3072,768]{2,1,0:T(8,128)}, f32[1,768]{1,0:T(1,128)S(1)}) conditional(s32[]{:T(128)} %convert_element_type.320, (f32[1,768,3072]{2,1,0:T(8,128)}, f32[1,3072,768]{2,1,0:T(8,128)}, f32[1,768]{1,0:T(1,128)S(1)}) %tuple.109, (pred[]{:T(512)}, s32[]{:T(128)}, ...), branch_computations={%region_9.9_spmd, %region_10.13_spmd} | conditional | flops 24277159936 | bytes 199846112 | solution.py:149
  2283.8 66.1 %conditional.15 = (bf16[1024,768]{1,0:T(8,128)(2,1)}, f32[1,768,3072]{2,1,0:T(8,128)}, f32[1,3072,768]{2,1,0:T(8,128)}, f32[1,768]{1,0:T(1,128)S(1)}) conditional(s32[]{:T(128)} %convert_element_type.321, (f32[1,768,3072]{2,1,0:T(8,128)}, f32[1,3072,768]{2,1,0:T(8,128)}, f32[1,768]{1,0:T(1,128)S(1)}) %tuple.111, (s32[]{:T(128)}, ...), branch_computations={%region_14.14_spmd, %region_15.18_spmd.clone} | conditional | flops 24278732800 | bytes 207698176 | solution.py:150
  2352.5 66.3 %conditional.14 = (bf16[1024,768]{1,0:T(8,128)(2,1)S(1)}, f32[1,768,3072]{2,1,0:T(8,128)}, f32[1,3072,768]{2,1,0:T(8,128)}, f32[1,768]{1,0:T(1,128)S(1)}) conditional(s32[]{:T(128)} %convert_element_type.320, (f32[1,768,3072]{2,1,0:T(8,128)}, f32[1,3072,768]{2,1,0:T(8,128)}, f32[1,768]{1,0:T(1,128)S(1)}) %tuple.109, (pred[]{:T(512)}, s32[]{:T(128)}, ...), branch_computations={%region_9.9_spmd, %region_10.13_spmd} | conditional | flops 24277159936 | bytes 199846112 | solution.py:149
  2442.5 65.8 %conditional.15 = (bf16[1024,768]{1,0:T(8,128)(2,1)}, f32[1,768,3072]{2,1,0:T(8,128)}, f32[1,3072,768]{2,1,0:T(8,128)}, f32[1,768]{1,0:T(1,128)S(1)}) conditional(s32[]{:T(128)} %convert_element_type.321, (f32[1,768,3072]{2,1,0:T(8,128)}, f32[1,3072,768]{2,1,0:T(8,128)}, f32[1,768]{1,0:T(1,128)S(1)}) %tuple.111, (s32[]{:T(128)}, ...), branch_computations={%region_14.14_spmd, %region_15.18_spmd.clone} | conditional | flops 24278732800 | bytes 207698176 | solution.py:150
  2510.9 66.6 %conditional.14 = (bf16[1024,768]{1,0:T(8,128)(2,1)S(1)}, f32[1,768,3072]{2,1,0:T(8,128)}, f32[1,3072,768]{2,1,0:T(8,128)}, f32[1,768]{1,0:T(1,128)S(1)}) conditional(s32[]{:T(128)} %convert_element_type.320, (f32[1,768,3072]{2,1,0:T(8,128)}, f32[1,3072,768]{2,1,0:T(8,128)}, f32[1,768]{1,0:T(1,128)S(1)}) %tuple.109, (pred[]{:T(512)}, s32[]{:T(128)}, ...), branch_computations={%region_9.9_spmd, %region_10.13_spmd} | conditional | flops 24277159936 | bytes 199846112 | solution.py:149
  2600.9 66.1 %conditional.15 = (bf16[1024,768]{1,0:T(8,128)(2,1)}, f32[1,768,3072]{2,1,0:T(8,128)}, f32[1,3072,768]{2,1,0:T(8,128)}, f32[1,768]{1,0:T(1,128)S(1)}) conditional(s32[]{:T(128)} %convert_element_type.321, (f32[1,768,3072]{2,1,0:T(8,128)}, f32[1,3072,768]{2,1,0:T(8,128)}, f32[1,768]{1,0:T(1,128)S(1)}) %tuple.111, (s32[]{:T(128)}, ...), branch_computations={%region_14.14_spmd, %region_15.18_spmd.clone} | conditional | flops 24278732800 | bytes 207698176 | solution.py:150
  2669.6 66.0 %conditional.14 = (bf16[1024,768]{1,0:T(8,128)(2,1)S(1)}, f32[1,768,3072]{2,1,0:T(8,128)}, f32[1,3072,768]{2,1,0:T(8,128)}, f32[1,768]{1,0:T(1,128)S(1)}) conditional(s32[]{:T(128)} %convert_element_type.320, (f32[1,768,3072]{2,1,0:T(8,128)}, f32[1,3072,768]{2,1,0:T(8,128)}, f32[1,768]{1,0:T(1,128)S(1)}) %tuple.109, (pred[]{:T(512)}, s32[]{:T(128)}, ...), branch_computations={%region_9.9_spmd, %region_10.13_spmd} | conditional | flops 24277159936 | bytes 199846112 | solution.py:149
  2759.1 66.1 %conditional.15 = (bf16[1024,768]{1,0:T(8,128)(2,1)}, f32[1,768,3072]{2,1,0:T(8,128)}, f32[1,3072,768]{2,1,0:T(8,128)}, f32[1,768]{1,0:T(1,128)S(1)}) conditional(s32[]{:T(128)} %convert_element_type.321, (f32[1,768,3072]{2,1,0:T(8,128)}, f32[1,3072,768]{2,1,0:T(8,128)}, f32[1,768]{1,0:T(1,128)S(1)}) %tuple.111, (s32[]{:T(128)}, ...), branch_computations={%region_14.14_spmd, %region_15.18_spmd.clone} | conditional | flops 24278732800 | bytes 207698176 | solution.py:150
  2827.8 66.3 %conditional.14 = (bf16[1024,768]{1,0:T(8,128)(2,1)S(1)}, f32[1,768,3072]{2,1,0:T(8,128)}, f32[1,3072,768]{2,1,0:T(8,128)}, f32[1,768]{1,0:T(1,128)S(1)}) conditional(s32[]{:T(128)} %convert_element_type.320, (f32[1,768,3072]{2,1,0:T(8,128)}, f32[1,3072,768]{2,1,0:T(8,128)}, f32[1,768]{1,0:T(1,128)S(1)}) %tuple.109, (pred[]{:T(512)}, s32[]{:T(128)}, ...), branch_computations={%region_9.9_spmd, %region_10.13_spmd} | conditional | flops 24277159936 | bytes 199846112 | solution.py:149
  2986.2 66.6 %conditional.14 = (bf16[1024,768]{1,0:T(8,128)(2,1)S(1)}, f32[1,768,3072]{2,1,0:T(8,128)}, f32[1,3072,768]{2,1,0:T(8,128)}, f32[1,768]{1,0:T(1,128)S(1)}) conditional(s32[]{:T(128)} %convert_element_type.320, (f32[1,768,3072]{2,1,0:T(8,128)}, f32[1,3072,768]{2,1,0:T(8,128)}, f32[1,768]{1,0:T(1,128)S(1)}) %tuple.109, (pred[]{:T(512)}, s32[]{:T(128)}, ...), branch_computations={%region_9.9_spmd, %region_10.13_spmd} | conditional | flops 24277159936 | bytes 199846112 | solution.py:149
  3076.2 66.1 %conditional.15 = (bf16[1024,768]{1,0:T(8,128)(2,1)}, f32[1,768,3072]{2,1,0:T(8,128)}, f32[1,3072,768]{2,1,0:T(8,128)}, f32[1,768]{1,0:T(1,128)S(1)}) conditional(s32[]{:T(128)} %convert_element_type.321, (f32[1,768,3072]{2,1,0:T(8,128)}, f32[1,3072,768]{2,1,0:T(8,128)}, f32[1,768]{1,0:T(1,128)S(1)}) %tuple.111, (s32[]{:T(128)}, ...), branch_computations={%region_14.14_spmd, %region_15.18_spmd.clone} | conditional | flops 24278732800 | bytes 207698176 | solution.py:150
  3144.9 66.0 %conditional.14 = (bf16[1024,768]{1,0:T(8,128)(2,1)S(1)}, f32[1,768,3072]{2,1,0:T(8,128)}, f32[1,3072,768]{2,1,0:T(8,128)}, f32[1,768]{1,0:T(1,128)S(1)}) conditional(s32[]{:T(128)} %convert_element_type.320, (f32[1,768,3072]{2,1,0:T(8,128)}, f32[1,3072,768]{2,1,0:T(8,128)}, f32[1,768]{1,0:T(1,128)S(1)}) %tuple.109, (pred[]{:T(512)}, s32[]{:T(128)}, ...), branch_computations={%region_9.9_spmd, %region_10.13_spmd} | conditional | flops 24277159936 | bytes 199846112 | solution.py:149
  3234.4 66.1 %conditional.15 = (bf16[1024,768]{1,0:T(8,128)(2,1)}, f32[1,768,3072]{2,1,0:T(8,128)}, f32[1,3072,768]{2,1,0:T(8,128)}, f32[1,768]{1,0:T(1,128)S(1)}) conditional(s32[]{:T(128)} %convert_element_type.321, (f32[1,768,3072]{2,1,0:T(8,128)}, f32[1,3072,768]{2,1,0:T(8,128)}, f32[1,768]{1,0:T(1,128)S(1)}) %tuple.111, (s32[]{:T(128)}, ...), branch_computations={%region_14.14_spmd, %region_15.18_spmd.clone} | conditional | flops 24278732800 | bytes 207698176 | solution.py:150
  3303.1 66.3 %conditional.14 = (bf16[1024,768]{1,0:T(8,128)(2,1)S(1)}, f32[1,768,3072]{2,1,0:T(8,128)}, f32[1,3072,768]{2,1,0:T(8,128)}, f32[1,768]{1,0:T(1,128)S(1)}) conditional(s32[]{:T(128)} %convert_element_type.320, (f32[1,768,3072]{2,1,0:T(8,128)}, f32[1,3072,768]{2,1,0:T(8,128)}, f32[1,768]{1,0:T(1,128)S(1)}) %tuple.109, (pred[]{:T(512)}, s32[]{:T(128)}, ...), branch_computations={%region_9.9_spmd, %region_10.13_spmd} | conditional | flops 24277159936 | bytes 199846112 | solution.py:149
  3461.5 66.6 %conditional.14 = (bf16[1024,768]{1,0:T(8,128)(2,1)S(1)}, f32[1,768,3072]{2,1,0:T(8,128)}, f32[1,3072,768]{2,1,0:T(8,128)}, f32[1,768]{1,0:T(1,128)S(1)}) conditional(s32[]{:T(128)} %convert_element_type.320, (f32[1,768,3072]{2,1,0:T(8,128)}, f32[1,3072,768]{2,1,0:T(8,128)}, f32[1,768]{1,0:T(1,128)S(1)}) %tuple.109, (pred[]{:T(512)}, s32[]{:T(128)}, ...), branch_computations={%region_9.9_spmd, %region_10.13_spmd} | conditional | flops 24277159936 | bytes 199846112 | solution.py:149
  3551.4 66.1 %conditional.15 = (bf16[1024,768]{1,0:T(8,128)(2,1)}, f32[1,768,3072]{2,1,0:T(8,128)}, f32[1,3072,768]{2,1,0:T(8,128)}, f32[1,768]{1,0:T(1,128)S(1)}) conditional(s32[]{:T(128)} %convert_element_type.321, (f32[1,768,3072]{2,1,0:T(8,128)}, f32[1,3072,768]{2,1,0:T(8,128)}, f32[1,768]{1,0:T(1,128)S(1)}) %tuple.111, (s32[]{:T(128)}, ...), branch_computations={%region_14.14_spmd, %region_15.18_spmd.clone} | conditional | flops 24278732800 | bytes 207698176 | solution.py:150
  3620.2 66.0 %conditional.14 = (bf16[1024,768]{1,0:T(8,128)(2,1)S(1)}, f32[1,768,3072]{2,1,0:T(8,128)}, f32[1,3072,768]{2,1,0:T(8,128)}, f32[1,768]{1,0:T(1,128)S(1)}) conditional(s32[]{:T(128)} %convert_element_type.320, (f32[1,768,3072]{2,1,0:T(8,128)}, f32[1,3072,768]{2,1,0:T(8,128)}, f32[1,768]{1,0:T(1,128)S(1)}) %tuple.109, (pred[]{:T(512)}, s32[]{:T(128)}, ...), branch_computations={%region_9.9_spmd, %region_10.13_spmd} | conditional | flops 24277159936 | bytes 199846112 | solution.py:149
  3709.6 66.1 %conditional.15 = (bf16[1024,768]{1,0:T(8,128)(2,1)}, f32[1,768,3072]{2,1,0:T(8,128)}, f32[1,3072,768]{2,1,0:T(8,128)}, f32[1,768]{1,0:T(1,128)S(1)}) conditional(s32[]{:T(128)} %convert_element_type.321, (f32[1,768,3072]{2,1,0:T(8,128)}, f32[1,3072,768]{2,1,0:T(8,128)}, f32[1,768]{1,0:T(1,128)S(1)}) %tuple.111, (s32[]{:T(128)}, ...), branch_computations={%region_14.14_spmd, %region_15.18_spmd.clone} | conditional | flops 24278732800 | bytes 207698176 | solution.py:150
  3778.4 66.3 %conditional.14 = (bf16[1024,768]{1,0:T(8,128)(2,1)S(1)}, f32[1,768,3072]{2,1,0:T(8,128)}, f32[1,3072,768]{2,1,0:T(8,128)}, f32[1,768]{1,0:T(1,128)S(1)}) conditional(s32[]{:T(128)} %convert_element_type.320, (f32[1,768,3072]{2,1,0:T(8,128)}, f32[1,3072,768]{2,1,0:T(8,128)}, f32[1,768]{1,0:T(1,128)S(1)}) %tuple.109, (pred[]{:T(512)}, s32[]{:T(128)}, ...), branch_computations={%region_9.9_spmd, %region_10.13_spmd} | conditional | flops 24277159936 | bytes 199846112 | solution.py:149
  4011.6 66.1 %conditional.15 = (bf16[1024,768]{1,0:T(8,128)(2,1)}, f32[1,768,3072]{2,1,0:T(8,128)}, f32[1,3072,768]{2,1,0:T(8,128)}, f32[1,768]{1,0:T(1,128)S(1)}) conditional(s32[]{:T(128)} %convert_element_type.321, (f32[1,768,3072]{2,1,0:T(8,128)}, f32[1,3072,768]{2,1,0:T(8,128)}, f32[1,768]{1,0:T(1,128)S(1)}) %tuple.111, (s32[]{:T(128)}, ...), branch_computations={%region_14.14_spmd, %region_15.18_spmd.clone} | conditional | flops 24278732800 | bytes 207698176 | solution.py:150
  4109.7 66.2 %conditional.15 = (bf16[1024,768]{1,0:T(8,128)(2,1)}, f32[1,768,3072]{2,1,0:T(8,128)}, f32[1,3072,768]{2,1,0:T(8,128)}, f32[1,768]{1,0:T(1,128)S(1)}) conditional(s32[]{:T(128)} %convert_element_type.321, (f32[1,768,3072]{2,1,0:T(8,128)}, f32[1,3072,768]{2,1,0:T(8,128)}, f32[1,768]{1,0:T(1,128)S(1)}) %tuple.111, (s32[]{:T(128)}, ...), branch_computations={%region_14.14_spmd, %region_15.18_spmd.clone} | conditional | flops 24278732800 | bytes 207698176 | solution.py:150
  (1554 shorter events, 4971.8 us)
Async XLA Ops:
  79.5 39.5 collective-permute-start
  210.9 37.6 collective-permute-start.1
  270.0 32.7 collective-permute-start.1
  388.1 32.7 collective-permute-start.1
  683.4 32.6 collective-permute-start.1
  860.5 32.7 collective-permute-start.1
  919.6 32.7 collective-permute-start.1
  1037.7 32.7 collective-permute-start.1
  1164.0 33.4 collective-permute-start.1
  1337.0 57.3 %collective-permute-start.3 = (bf16[1024,768]{1,0:T(8,128)(2,1)}, bf16[1024,768]{1,0:T(8,128)(2,1)}, u32[]{:S(2)}, u32[]{:S(2)}) collective-permute-start(bf16[1024,768]{1,0:T(8,128)(2,1)} %get-tuple-element.972), channel_id=1, source_target_pairs={{1,0},{2,1},{3,2},{5,4},{6,5},{7,6}} | collective-permute-start | bytes 4718600 | tf_op jit(solution)/shard_map/while/body/eval_jaxpr/ppermute | solution.py:153
  1377.6 96.8 %collective-permute-start.2 = (bf16[1024,768]{1,0:T(8,128)(2,1)S(1)}, bf16[1024,768]{1,0:T(8,128)(2,1)S(1)}, u32[]{:S(2)}, u32[]{:S(2)}) collective-permute-start(bf16[1024,768]{1,0:T(8,128)(2,1)S(1)} %get-tuple-element.971), channel_id=1, source_target_pairs={{0,1},{1,2},{2,3},{4,5},{5,6},{6,7}} | collective-permute-start | bytes 4718600 | tf_op jit(solution)/shard_map/while/body/eval_jaxpr/ppermute | solution.py:152
  1477.0 79.7 %collective-permute-start.3 = (bf16[1024,768]{1,0:T(8,128)(2,1)}, bf16[1024,768]{1,0:T(8,128)(2,1)}, u32[]{:S(2)}, u32[]{:S(2)}) collective-permute-start(bf16[1024,768]{1,0:T(8,128)(2,1)} %get-tuple-element.972), channel_id=1, source_target_pairs={{1,0},{2,1},{3,2},{5,4},{6,5},{7,6}} | collective-permute-start | bytes 4718600 | tf_op jit(solution)/shard_map/while/body/eval_jaxpr/ppermute | solution.py:153
  1588.4 72.9 %collective-permute-start.3 = (bf16[1024,768]{1,0:T(8,128)(2,1)}, bf16[1024,768]{1,0:T(8,128)(2,1)}, u32[]{:S(2)}, u32[]{:S(2)}) collective-permute-start(bf16[1024,768]{1,0:T(8,128)(2,1)} %get-tuple-element.972), channel_id=1, source_target_pairs={{1,0},{2,1},{3,2},{5,4},{6,5},{7,6}} | collective-permute-start | bytes 4718600 | tf_op jit(solution)/shard_map/while/body/eval_jaxpr/ppermute | solution.py:153
  1691.2 112.6 %collective-permute-start.3 = (bf16[1024,768]{1,0:T(8,128)(2,1)}, bf16[1024,768]{1,0:T(8,128)(2,1)}, u32[]{:S(2)}, u32[]{:S(2)}) collective-permute-start(bf16[1024,768]{1,0:T(8,128)(2,1)} %get-tuple-element.972), channel_id=1, source_target_pairs={{1,0},{2,1},{3,2},{5,4},{6,5},{7,6}} | collective-permute-start | bytes 4718600 | tf_op jit(solution)/shard_map/while/body/eval_jaxpr/ppermute | solution.py:153
  1760.0 46.9 %collective-permute-start.2 = (bf16[1024,768]{1,0:T(8,128)(2,1)S(1)}, bf16[1024,768]{1,0:T(8,128)(2,1)S(1)}, u32[]{:S(2)}, u32[]{:S(2)}) collective-permute-start(bf16[1024,768]{1,0:T(8,128)(2,1)S(1)} %get-tuple-element.971), channel_id=1, source_target_pairs={{0,1},{1,2},{2,3},{4,5},{5,6},{6,7}} | collective-permute-start | bytes 4718600 | tf_op jit(solution)/shard_map/while/body/eval_jaxpr/ppermute | solution.py:152
  1874.6 72.5 %collective-permute-start.3 = (bf16[1024,768]{1,0:T(8,128)(2,1)}, bf16[1024,768]{1,0:T(8,128)(2,1)}, u32[]{:S(2)}, u32[]{:S(2)}) collective-permute-start(bf16[1024,768]{1,0:T(8,128)(2,1)} %get-tuple-element.972), channel_id=1, source_target_pairs={{1,0},{2,1},{3,2},{5,4},{6,5},{7,6}} | collective-permute-start | bytes 4718600 | tf_op jit(solution)/shard_map/while/body/eval_jaxpr/ppermute | solution.py:153
  2033.0 72.9 %collective-permute-start.3 = (bf16[1024,768]{1,0:T(8,128)(2,1)}, bf16[1024,768]{1,0:T(8,128)(2,1)}, u32[]{:S(2)}, u32[]{:S(2)}) collective-permute-start(bf16[1024,768]{1,0:T(8,128)(2,1)} %get-tuple-element.972), channel_id=1, source_target_pairs={{1,0},{2,1},{3,2},{5,4},{6,5},{7,6}} | collective-permute-start | bytes 4718600 | tf_op jit(solution)/shard_map/while/body/eval_jaxpr/ppermute | solution.py:153
  2191.7 72.3 %collective-permute-start.3 = (bf16[1024,768]{1,0:T(8,128)(2,1)}, bf16[1024,768]{1,0:T(8,128)(2,1)}, u32[]{:S(2)}, u32[]{:S(2)}) collective-permute-start(bf16[1024,768]{1,0:T(8,128)(2,1)} %get-tuple-element.972), channel_id=1, source_target_pairs={{1,0},{2,1},{3,2},{5,4},{6,5},{7,6}} | collective-permute-start | bytes 4718600 | tf_op jit(solution)/shard_map/while/body/eval_jaxpr/ppermute | solution.py:153
  2349.9 72.5 %collective-permute-start.3 = (bf16[1024,768]{1,0:T(8,128)(2,1)}, bf16[1024,768]{1,0:T(8,128)(2,1)}, u32[]{:S(2)}, u32[]{:S(2)}) collective-permute-start(bf16[1024,768]{1,0:T(8,128)(2,1)} %get-tuple-element.972), channel_id=1, source_target_pairs={{1,0},{2,1},{3,2},{5,4},{6,5},{7,6}} | collective-permute-start | bytes 4718600 | tf_op jit(solution)/shard_map/while/body/eval_jaxpr/ppermute | solution.py:153
  2508.3 72.9 %collective-permute-start.3 = (bf16[1024,768]{1,0:T(8,128)(2,1)}, bf16[1024,768]{1,0:T(8,128)(2,1)}, u32[]{:S(2)}, u32[]{:S(2)}) collective-permute-start(bf16[1024,768]{1,0:T(8,128)(2,1)} %get-tuple-element.972), channel_id=1, source_target_pairs={{1,0},{2,1},{3,2},{5,4},{6,5},{7,6}} | collective-permute-start | bytes 4718600 | tf_op jit(solution)/shard_map/while/body/eval_jaxpr/ppermute | solution.py:153
  2667.0 72.3 %collective-permute-start.3 = (bf16[1024,768]{1,0:T(8,128)(2,1)}, bf16[1024,768]{1,0:T(8,128)(2,1)}, u32[]{:S(2)}, u32[]{:S(2)}) collective-permute-start(bf16[1024,768]{1,0:T(8,128)(2,1)} %get-tuple-element.972), channel_id=1, source_target_pairs={{1,0},{2,1},{3,2},{5,4},{6,5},{7,6}} | collective-permute-start | bytes 4718600 | tf_op jit(solution)/shard_map/while/body/eval_jaxpr/ppermute | solution.py:153
  2825.2 72.5 %collective-permute-start.3 = (bf16[1024,768]{1,0:T(8,128)(2,1)}, bf16[1024,768]{1,0:T(8,128)(2,1)}, u32[]{:S(2)}, u32[]{:S(2)}) collective-permute-start(bf16[1024,768]{1,0:T(8,128)(2,1)} %get-tuple-element.972), channel_id=1, source_target_pairs={{1,0},{2,1},{3,2},{5,4},{6,5},{7,6}} | collective-permute-start | bytes 4718600 | tf_op jit(solution)/shard_map/while/body/eval_jaxpr/ppermute | solution.py:153
  2983.6 72.9 %collective-permute-start.3 = (bf16[1024,768]{1,0:T(8,128)(2,1)}, bf16[1024,768]{1,0:T(8,128)(2,1)}, u32[]{:S(2)}, u32[]{:S(2)}) collective-permute-start(bf16[1024,768]{1,0:T(8,128)(2,1)} %get-tuple-element.972), channel_id=1, source_target_pairs={{1,0},{2,1},{3,2},{5,4},{6,5},{7,6}} | collective-permute-start | bytes 4718600 | tf_op jit(solution)/shard_map/while/body/eval_jaxpr/ppermute | solution.py:153
  3142.3 72.3 %collective-permute-start.3 = (bf16[1024,768]{1,0:T(8,128)(2,1)}, bf16[1024,768]{1,0:T(8,128)(2,1)}, u32[]{:S(2)}, u32[]{:S(2)}) collective-permute-start(bf16[1024,768]{1,0:T(8,128)(2,1)} %get-tuple-element.972), channel_id=1, source_target_pairs={{1,0},{2,1},{3,2},{5,4},{6,5},{7,6}} | collective-permute-start | bytes 4718600 | tf_op jit(solution)/shard_map/while/body/eval_jaxpr/ppermute | solution.py:153
  3300.4 72.5 %collective-permute-start.3 = (bf16[1024,768]{1,0:T(8,128)(2,1)}, bf16[1024,768]{1,0:T(8,128)(2,1)}, u32[]{:S(2)}, u32[]{:S(2)}) collective-permute-start(bf16[1024,768]{1,0:T(8,128)(2,1)} %get-tuple-element.972), channel_id=1, source_target_pairs={{1,0},{2,1},{3,2},{5,4},{6,5},{7,6}} | collective-permute-start | bytes 4718600 | tf_op jit(solution)/shard_map/while/body/eval_jaxpr/ppermute | solution.py:153
  3458.9 72.9 %collective-permute-start.3 = (bf16[1024,768]{1,0:T(8,128)(2,1)}, bf16[1024,768]{1,0:T(8,128)(2,1)}, u32[]{:S(2)}, u32[]{:S(2)}) collective-permute-start(bf16[1024,768]{1,0:T(8,128)(2,1)} %get-tuple-element.972), channel_id=1, source_target_pairs={{1,0},{2,1},{3,2},{5,4},{6,5},{7,6}} | collective-permute-start | bytes 4718600 | tf_op jit(solution)/shard_map/while/body/eval_jaxpr/ppermute | solution.py:153
  3617.5 72.3 %collective-permute-start.3 = (bf16[1024,768]{1,0:T(8,128)(2,1)}, bf16[1024,768]{1,0:T(8,128)(2,1)}, u32[]{:S(2)}, u32[]{:S(2)}) collective-permute-start(bf16[1024,768]{1,0:T(8,128)(2,1)} %get-tuple-element.972), channel_id=1, source_target_pairs={{1,0},{2,1},{3,2},{5,4},{6,5},{7,6}} | collective-permute-start | bytes 4718600 | tf_op jit(solution)/shard_map/while/body/eval_jaxpr/ppermute | solution.py:153
  3775.7 72.5 %collective-permute-start.3 = (bf16[1024,768]{1,0:T(8,128)(2,1)}, bf16[1024,768]{1,0:T(8,128)(2,1)}, u32[]{:S(2)}, u32[]{:S(2)}) collective-permute-start(bf16[1024,768]{1,0:T(8,128)(2,1)} %get-tuple-element.972), channel_id=1, source_target_pairs={{1,0},{2,1},{3,2},{5,4},{6,5},{7,6}} | collective-permute-start | bytes 4718600 | tf_op jit(solution)/shard_map/while/body/eval_jaxpr/ppermute | solution.py:153
  3934.2 72.9 %collective-permute-start.3 = (bf16[1024,768]{1,0:T(8,128)(2,1)}, bf16[1024,768]{1,0:T(8,128)(2,1)}, u32[]{:S(2)}, u32[]{:S(2)}) collective-permute-start(bf16[1024,768]{1,0:T(8,128)(2,1)} %get-tuple-element.972), channel_id=1, source_target_pairs={{1,0},{2,1},{3,2},{5,4},{6,5},{7,6}} | collective-permute-start | bytes 4718600 | tf_op jit(solution)/shard_map/while/body/eval_jaxpr/ppermute | solution.py:153
  3943.1 66.9 %collective-permute-start.2 = (bf16[1024,768]{1,0:T(8,128)(2,1)S(1)}, bf16[1024,768]{1,0:T(8,128)(2,1)S(1)}, u32[]{:S(2)}, u32[]{:S(2)}) collective-permute-start(bf16[1024,768]{1,0:T(8,128)(2,1)S(1)} %get-tuple-element.971), channel_id=1, source_target_pairs={{0,1},{1,2},{2,3},{4,5},{5,6},{6,7}} | collective-permute-start | bytes 4718600 | tf_op jit(solution)/shard_map/while/body/eval_jaxpr/ppermute | solution.py:152
  4214.1 79.0 %collective-permute-start.3 = (bf16[1024,768]{1,0:T(8,128)(2,1)}, bf16[1024,768]{1,0:T(8,128)(2,1)}, u32[]{:S(2)}, u32[]{:S(2)}) collective-permute-start(bf16[1024,768]{1,0:T(8,128)(2,1)} %get-tuple-element.972), channel_id=1, source_target_pairs={{1,0},{2,1},{3,2},{5,4},{6,5},{7,6}} | collective-permute-start | bytes 4718600 | tf_op jit(solution)/shard_map/while/body/eval_jaxpr/ppermute | solution.py:153
  4316.4 63.1 %collective-permute-start.2 = (bf16[1024,768]{1,0:T(8,128)(2,1)S(1)}, bf16[1024,768]{1,0:T(8,128)(2,1)S(1)}, u32[]{:S(2)}, u32[]{:S(2)}) collective-permute-start(bf16[1024,768]{1,0:T(8,128)(2,1)S(1)} %get-tuple-element.971), channel_id=1, source_target_pairs={{0,1},{1,2},{2,3},{4,5},{5,6},{6,7}} | collective-permute-start | bytes 4718600 | tf_op jit(solution)/shard_map/while/body/eval_jaxpr/ppermute | solution.py:152
  (290 other events, 5828.1 us)
where the time goes:
time: 4440 us; the launch traced here: 4420 us
  matrix products  2390 us (54%)
  waiting for transfers between devices  649 us (15%)
  other arithmetic  509 us (11%)
  starting transfers between devices  486 us (11%)
  local copies, waits for them, and re-layouts  231 us (5%)
  loops' own time  147 us (3%)
    dot_general x32, matrix products, layer_forward(): out_f32 = jnp.dot(hidden, second_w, preferred_element_type=jnp.float32)  487 us
    dot_general x32, matrix products, layer_backward(): jnp.einsum('td,fd->tf', grad_h, second_w, preferred_element_type=jnp.floa...  486 us
    dot_general x32, matrix products, layer_backward(): jnp.einsum('tf,td->fd', hidden, grad_h, preferred_element_type=jnp.float32)  453 us
    ppermute x23, waiting for transfers between devices, backward_tick(): recv_up = lax.ppermute(grad_up_out, 'stage', down_perm)  383 us
    dot_general x32, matrix products, layer_backward(): jnp.einsum('tf,df->td', grad_pre, first_w, preferred_element_type=jnp.flo...  375 us
    dot_general x32, matrix products, layer_backward(): pre_act = jnp.dot(normed, first_w, preferred_element_type=jnp.float32)  347 us
    dot_general x32, matrix products, layer_backward(): jnp.einsum('td,tf->df', normed, grad_pre, preferred_element_type=jnp.floa...  236 us
    ppermute x23, waiting for transfers between devices, forward_tick(): recv_down = lax.ppermute(out_down, 'stage', down_perm)  183 us
  transfers between devices with their start and end apart: 92, of which 57 were waited for; matrix products, arithmetic and copies ran while one was open for 37% of the time, Pallas kernels for 0%

commit v1 on v0

v1 whole, which is shorter than its diff:
```python
import functools

import jax
import jax.numpy as jnp
from jax import lax
from jax.experimental import pallas as pl
from jax.experimental.pallas import tpu as pltpu
from jax.sharding import PartitionSpec as P

EPSILON = 1e-6
GELU_A = 0.7978845608028654
GELU_B = 0.7978845608028654 * 0.044715
CHUNK = 512
F_FWD = 512
F_BWD = 256
N_BLK = 256
VMEM_LIMIT = 67_043_328
BF16 = jnp.bfloat16
F32 = jnp.float32


def dot(a, b):
    return jnp.dot(a, b, preferred_element_type=F32)


def dot_rt(a, b):
    return lax.dot_general(a, b, (((1,), (1,)), ((), ())), preferred_element_type=F32)


def inverse_rms(x_f32):
    return lax.rsqrt(jnp.mean(x_f32 * x_f32, axis=-1, keepdims=True) + EPSILON)


def gelu_of(a):
    t = jnp.tanh(a * (GELU_A + GELU_B * (a * a)))
    h = 0.5 * a
    return h + h * t


def gelu_and_slope(a):
    a2 = a * a
    t = jnp.tanh(a * (GELU_A + GELU_B * a2))
    h = 0.5 * a
    slope = (0.5 + 0.5 * t) + h * (1.0 - t * t) * (GELU_A + (3.0 * GELU_B) * a2)
    return h + h * t, slope


def fold_rows(v):
    return jnp.sum(v.reshape(v.shape[0] // 8, 8, v.shape[1]), axis=0)


def enter(stage, stages):
    barrier = pltpu.get_barrier_semaphore()
    for step in (1, stages - 1):
        pl.semaphore_signal(barrier, inc=1, device_id={"stage": lax.rem(stage + step, stages)},
                            device_id_type=pl.DeviceIdType.MESH)
    pl.semaphore_wait(barrier, 2)


def run_schedule(stage, stages, count, lag, most_lag, land, outs, send, recv, issue, first_half, second_half,
                 finish, wait_finish, midway):
    last = stages - 1

    def place(k):
        p = lax.rem(k, 2)
        c = lax.div(k, 2) - p * lag
        return p, c, (c >= 0) & (c < count)

    def hop(p, c):
        return pltpu.make_async_remote_copy(
            src_ref=outs.at[p], dst_ref=land.at[p, c], send_sem=send.at[p], recv_sem=recv.at[p, c],
            device_id={"stage": stage + 1 - 2 * p}, device_id_type=pl.DeviceIdType.MESH)

    def turn(c):
        return pltpu.make_async_copy(outs.at[0], land.at[1, c], recv.at[1, c])

    def leaves(p):
        return ((p == 0) & (stage < last)) | ((p == 1) & (stage > 0))

    def arrived(p, c):
        pltpu.make_async_copy(outs.at[p], land.at[p, c], recv.at[p, c]).wait()

    def step(k, carry):
        p, c, valid = place(k)
        p_next, c_next, valid_next = place(k + 1)

        @pl.when(valid)
        def _():
            first_half(p, c)

        @pl.when(valid_next)
        def _():
            @pl.when((p_next == 1) | (stage > 0))
            def _():
                arrived(p_next, c_next)
            issue(p_next, c_next)

        midway(k)

        @pl.when(valid)
        def _():
            @pl.when((c >= 1) & leaves(p))
            def _():
                hop(p, c).wait_send()

            @pl.when((c >= 1) & (p == 1) & (stage == 0))
            def _():
                wait_finish(c)
            second_half(p, c)

            @pl.when(leaves(p))
            def _():
                hop(p, c).start()

            @pl.when((p == 0) & (stage == last))
            def _():
                turn(c).start()

            @pl.when((p == 1) & (stage == 0))
            def _():
                finish(c)
        return carry

    @pl.when(stage > 0)
    def _():
        arrived(0, 0)
    issue(0, 0)
    lax.fori_loop(0, 2 * (count + most_lag), step, 0)

    @pl.when(stage < last)
    def _():
        hop(0, count - 1).wait_send()

    @pl.when(stage > 0)
    def _():
        hop(1, count - 1).wait_send()

    @pl.when(stage == 0)
    def _():
        wait_finish(count - 1)


def forward_kernel(stages, seed_scale, tokens, targets, w_in, w_out, gains, land, seeds, sse,
                   wi, wo, xs, outs, tgt, normed, hidden, w_sem, ld_sem, tgt_sem, fin_sem, send, recv):
    stage = lax.axis_index("stage")
    count, _, d_model = tokens.shape
    d_ff = wi.shape[2]
    lag = (stages - 1 - stage) * 3 + 1
    most_lag = (stages - 1) * 3 + 1
    loads = [pltpu.make_async_copy(w_in, wi, w_sem.at[0]), pltpu.make_async_copy(w_out, wo, w_sem.at[1])]
    for load in loads:
        load.start()
    sse[...] = jnp.zeros_like(sse)
    enter(stage, stages)

    def tgt_load(c):
        return pltpu.make_async_copy(targets.at[c], tgt, tgt_sem)

    def issue(p, c):
        @pl.when((p == 0) & (stage == 0))
        def _():
            pltpu.make_async_copy(tokens.at[c], xs.at[p], ld_sem.at[p]).start()

        @pl.when((p == 1) | (stage > 0))
        def _():
            pltpu.make_async_copy(land.at[p, c], xs.at[p], ld_sem.at[p]).start()

        @pl.when((p == 1) & (stage == 0))
        def _():
            tgt_load(c).start()

    for load in loads:
        load.wait()

    def first_half(p, c):
        pltpu.make_async_copy(land.at[p, c], xs.at[p], ld_sem.at[p]).wait()
        x = xs[p].astype(F32)
        normed[...] = (x * inverse_rms(x) * gains[p]).astype(BF16)
        for f in range(0, d_ff, F_FWD):
            a = dot(normed[...], wi[p, :, f:f + F_FWD])
            hidden[:, f:f + F_FWD] = gelu_of(a).astype(BF16)

    def second_half(p, c):
        for n in range(0, d_model, N_BLK):
            cols = slice(n, n + N_BLK)
            out = dot(hidden[...], wo[p, :, cols])
            outs[p, :, cols] = (xs[p, :, cols].astype(F32) + out).astype(BF16)

        @pl.when((p == 1) & (stage == 0))
        def _():
            tgt_load(c).wait()
            error = outs[1].astype(F32) - tgt[...].astype(F32)
            sse[...] += fold_rows(error * error)
            outs[1] = (error * seed_scale).astype(BF16)

    def seed_store(c):
        return pltpu.make_async_copy(outs.at[1], seeds.at[c], fin_sem)

    run_schedule(stage, stages, count, lag, most_lag, land, outs, send, recv, issue, first_half, second_half,
                 lambda c: seed_store(c).start(), lambda c: seed_store(c).wait(), lambda k: None)


def backward_kernel(stages, tokens, saved, seeds, w_in, w_out, gains, land, grad_in, grad_out_t, grad_gain,
                    wi, wo_first, wo_ring, acc_in, acc_out, xs, dhs, outs, normed, normed_t, dh_t, dn, hidden, da,
                    w_sem, ring_sem, x_sem, dh_sem, flush_sem, send, recv):
    stage = lax.axis_index("stage")
    count, _, d_model = tokens.shape
    d_ff = wi.shape[2]
    blocks = d_ff // F_BWD
    lag = ((stages - 1 - stage) * 5) // 2 + 1
    most_lag = ((stages - 1) * 5) // 2 + 1
    loads = [pltpu.make_async_copy(w_in, wi, w_sem.at[0]),
             pltpu.make_async_copy(w_out.at[0, pl.ds(0, F_BWD)], wo_first.at[0], w_sem.at[1]),
             pltpu.make_async_copy(w_out.at[1, pl.ds(0, F_BWD)], wo_first.at[1], w_sem.at[2])]
    for load in loads:
        load.start()
    grad_gain[...] = jnp.zeros_like(grad_gain)

    def clear(i, carry):
        rows = pl.ds(pl.multiple_of(i * 8, 8), 8)
        for row in range(2):
            acc_in[row, rows, :] = jnp.zeros((8, d_ff), F32)
            acc_out[row, rows, :] = jnp.zeros((8, d_ff), F32)
        return carry

    lax.fori_loop(0, d_model // 8, clear, 0)
    enter(stage, stages)

    def issue(p, c):
        @pl.when((p == 0) & (stage == 0))
        def _():
            pltpu.make_async_copy(seeds.at[c], dhs.at[p], dh_sem.at[p]).start()

        @pl.when((p == 1) | (stage > 0))
        def _():
            pltpu.make_async_copy(land.at[p, c], dhs.at[p], dh_sem.at[p]).start()

        @pl.when((p == 1) & (stage == 0))
        def _():
            pltpu.make_async_copy(tokens.at[c], xs.at[p], x_sem.at[p]).start()

        @pl.when((p == 0) | (stage > 0))
        def _():
            pltpu.make_async_copy(saved.at[1 - p, c], xs.at[p], x_sem.at[p]).start()

    for load in loads:
        load.wait()

    def ring_load(row, block):
        return pltpu.make_async_copy(w_out.at[row, pl.ds(block * F_BWD, F_BWD)], wo_ring.at[block % 3],
                                     ring_sem.at[block % 3])

    def weight_grads(row, block):
        cols = slice(block * F_BWD, (block + 1) * F_BWD)
        acc_out[row, :, cols] += dot(dh_t[...], hidden[block % 2])
        acc_in[row, :, cols] += dot(normed_t[...], da[:, cols])

    def first_half(p, c):
        row = 1 - p
        ring_load(row, 1).start()
        ring_load(row, 2).start()
        pltpu.make_async_copy(land.at[p, c], dhs.at[p], dh_sem.at[p]).wait()
        pltpu.make_async_copy(saved.at[1 - p, c], xs.at[p], x_sem.at[p]).wait()
        x = xs[p].astype(F32)
        n = (x * inverse_rms(x) * gains[row]).astype(BF16)
        normed[...] = n
        normed_t[...] = n.T
        dh_t[...] = dhs[p].T
        for block in range(blocks):
            cols = slice(block * F_BWD, (block + 1) * F_BWD)
            if block:
                ring_load(row, block).wait()
                if block + 2 < blocks:
                    ring_load(row, block + 2).start()
            wo_block = wo_ring[block % 3] if block else wo_first[row]
            du = dot_rt(dhs[p], wo_block)
            a = dot(normed[...], wi[row, :, cols])
            if block:
                weight_grads(row, block - 1)
            u, slope = gelu_and_slope(a)
            hidden[block % 2] = u.astype(BF16)
            da[:, cols] = (du * slope).astype(BF16)

    def second_half(p, c):
        row = 1 - p
        for n in range(0, d_model, N_BLK):
            dn[:, n:n + N_BLK] = dot_rt(da[...], wi[row, n:n + N_BLK, :])
        weight_grads(row, blocks - 1)
        x = xs[p].astype(F32)
        inv = inverse_rms(x)
        grad_n = dn[...]
        xr = x * inv
        grad_gain[row] += fold_rows(xr * grad_n)
        scaled = grad_n * gains[row]
        mean = jnp.mean(xr * scaled, axis=-1, keepdims=True)
        outs[p] = (dhs[p].astype(F32) + inv * (scaled - xr * mean)).astype(BF16)

    def flushes(row):
        return [pltpu.make_async_copy(acc_in.at[row], grad_in.at[row], flush_sem.at[0, row]),
                pltpu.make_async_copy(acc_out.at[row], grad_out_t.at[row], flush_sem.at[1, row])]

    def midway(k):
        @pl.when(k == 2 * count)
        def _():
            for flush in flushes(1):
                flush.start()

    run_schedule(stage, stages, count, lag, most_lag, land, outs, send, recv, issue, first_half, second_half,
                 lambda c: None, lambda c: None, midway)
    for flush in flushes(0):
        flush.start()
    for row in (1, 0):
        for flush in flushes(row):
            flush.wait()


def solution(mesh):
    stages = mesh.shape['stage']

    def device_step(tokens, targets, w_in, w_out, norm_gains):
        micro_count, tokens_mb, d_model = tokens.shape
        d_ff = w_in.shape[2]
        total = micro_count * tokens_mb
        count = total // CHUNK
        tokens = tokens.reshape(count, CHUNK, d_model)
        targets = targets.reshape(count, CHUNK, d_model)
        gains = norm_gains.reshape(2, 1, d_model)
        any_spec = pl.BlockSpec(memory_space=pl.ANY)
        vmem_spec = pl.BlockSpec(memory_space=pltpu.VMEM)
        dma = pltpu.SemaphoreType.DMA
        flops = 2 * 2 * total * d_model * d_ff
        land_shape = jax.ShapeDtypeStruct((2, count, CHUNK, d_model), BF16)

        saved, seeds, sse = pl.pallas_call(
            functools.partial(forward_kernel, stages, 2.0 / total),
            out_shape=(land_shape, jax.ShapeDtypeStruct((count, CHUNK, d_model), BF16),
                       jax.ShapeDtypeStruct((8, d_model), F32)),
            in_specs=[any_spec] * 4 + [vmem_spec],
            out_specs=(any_spec, any_spec, vmem_spec),
            scratch_shapes=[
                pltpu.VMEM((2, d_model, d_ff), BF16), pltpu.VMEM((2, d_ff, d_model), BF16),
                pltpu.VMEM((2, CHUNK, d_model), BF16), pltpu.VMEM((2, CHUNK, d_model), BF16),
                pltpu.VMEM((CHUNK, d_model), BF16), pltpu.VMEM((CHUNK, d_model), BF16),
                pltpu.VMEM((CHUNK, d_ff), BF16),
                dma((2,)), dma((2,)), dma, dma, dma((2,)), dma((2, count)),
            ],
            compiler_params=pltpu.CompilerParams(collective_id=0, has_side_effects=True,
                                                 vmem_limit_bytes=VMEM_LIMIT),
            cost_estimate=pl.CostEstimate(flops=2 * flops, bytes_accessed=10 ** 8, transcendentals=0),
        )(tokens, targets, w_in, w_out, gains)

        _, grad_in, grad_out_t, grad_gain = pl.pallas_call(
            functools.partial(backward_kernel, stages),
            out_shape=(land_shape, jax.ShapeDtypeStruct((2, d_model, d_ff), F32),
                       jax.ShapeDtypeStruct((2, d_model, d_ff), F32),
                       jax.ShapeDtypeStruct((2, 8, d_model), F32)),
            in_specs=[any_spec] * 5 + [vmem_spec],
            out_specs=(any_spec, any_spec, any_spec, vmem_spec),
            scratch_shapes=[
                pltpu.VMEM((2, d_model, d_ff), BF16),
                pltpu.VMEM((2, F_BWD, d_model), BF16), pltpu.VMEM((3, F_BWD, d_model), BF16),
                pltpu.VMEM((2, d_model, d_ff), F32), pltpu.VMEM((2, d_model, d_ff), F32),
                pltpu.VMEM((2, CHUNK, d_model), BF16), pltpu.VMEM((2, CHUNK, d_model), BF16),
                pltpu.VMEM((2, CHUNK, d_model), BF16),
                pltpu.VMEM((CHUNK, d_model), BF16),
                pltpu.VMEM((d_model, CHUNK), BF16), pltpu.VMEM((d_model, CHUNK), BF16),
                pltpu.VMEM((CHUNK, d_model), F32),
                pltpu.VMEM((2, CHUNK, F_BWD), BF16), pltpu.VMEM((CHUNK, d_ff), BF16),
                dma((3,)), dma((3,)), dma((2,)), dma((2,)), dma((2, 2)), dma((2,)), dma((2, count)),
            ],
            compiler_params=pltpu.CompilerParams(collective_id=1, has_side_effects=True,
                                                 vmem_limit_bytes=VMEM_LIMIT),
            cost_estimate=pl.CostEstimate(flops=5 * flops, bytes_accessed=10 ** 8, transcendentals=0),
        )(tokens, saved, seeds, w_in, w_out, gains)

        loss_value = lax.psum(jnp.sum(sse), 'stage') / (total * d_model)
        return grad_in, jnp.swapaxes(grad_out_t, 1, 2), jnp.sum(grad_gain, axis=1), loss_value.reshape(1)

    block_spec = P(('dp', 'stage'))
    return jax.shard_map(device_step, mesh=mesh,
                         in_specs=(P('dp'), P('dp'), P('stage'), P('stage'), P('stage')),
                         out_specs=(block_spec, block_spec, block_spec, P('dp')),
                         check_vma=False)
```

time: 4440 us -> 1840 us (0.41)
  the two profiles are of different devices: /device:TPU:6 before, /device:TPU:4 now
where the time goes in v1:
time: 1840 us
  Pallas kernels  1800 us (98%)
  local copies, waits for them, and re-layouts  32.9 us (2%)
    pallas_call x1, Pallas kernels, device_step(): pl.pallas_call(functools.partial(backward_kernel, stages), out_shape=(lan...  1270 us
    pallas_call x1, Pallas kernels, device_step(): pl.pallas_call(functools.partial(forward_kernel, stages, 2.0 / total), ou...  528 us

profile of v1, /device:TPU:4, one launch (start us, length us, event | category | flops | bytes accessed | tf_op | source)
XLA Modules:
  0.0 1840.8 jit_solution(1246701257262960979)
XLA Ops:
  0.6 1.3 reshape.22.gains
  1.9 528.1 %shard_map.84 = (bf16[2,32,512,768]{3,2,1,0:T(8,128)(2,1)}, bf16[32,512,768]{2,1,0:T(8,128)(2,1)}, f32[8,768]{1,0:T(8,128)}) custom-call(bf16[32,512,768]{2,1,0:T(8,128)(2,1)} %bitcast.6, bf16[32,512,768]{2,1,0:T(8,128)(2,1)} %bitcast.5, bf16[2,768,3072]{2,1,0:T(8,128)(2,1)} %w_in.3, bf16[2,3072,768]{2,1,0:T(8,128)(2,1)} %w_out.3, f32[2,1,768]{2,1,0:T(1,128)} %reshape.22.gains), custom_call_target="tpu_custom_call" | custom-call | flops 309237645312 | bytes 100000000 | tf_op jit(solution)/shard_map/pallas_call | solution.py:334
  530.1 1.3 reduce_sum.19
  531.4 6.4 psum.7
  538.4 1269.0 %shard_map.85 = (bf16[2,32,512,768]{3,2,1,0:T(8,128)(2,1)}, f32[2,768,3072]{2,1,0:T(8,128)}, f32[2,768,3072]{2,1,0:T(8,128)}, f32[2,8,768]{2,1,0:T(8,128)}) custom-call(bf16[32,512,768]{2,1,0:T(8,128)(2,1)} %bitcast.7, bf16[2,32,512,768]{3,2,1,0:T(8,128)(2,1)} %get-tuple-element.10.saved, bf16[32,512,768]{2,1,0:T(8,128)(2,1)} %get-tuple-element.11.seeds, ...), custom_call_target="tpu_custom_call" | custom-call | flops 773094113280 | bytes 100000000 | tf_op jit(solution)/shard_map/pallas_call | solution.py:352
  1807.4 0.0 copy-start
  1807.4 18.7 %copy.9 = f32[2,3072,768]{2,1,0:T(8,128)} copy(f32[2,3072,768]{1,2,0:T(8,128)} %bitcast.4) | data formatting | bytes 37748736
  1826.1 0.0 copy-done
  1826.1 0.6 reduce_sum.18
  1826.7 12.9 copy.11
Async XLA Ops:
  1807.4 18.7 %copy-start = (f32[2,8,768]{2,1,0:T(8,128)S(1)}, f32[2,8,768]{2,1,0:T(8,128)}, u32[]{:S(2)}) copy-start(f32[2,8,768]{2,1,0:T(8,128)} %get-tuple-element.14) | copy-start | bytes 147460

commit v2 on v0

v2 whole, which is shorter than its diff:
```python
import functools

import jax
import jax.numpy as jnp
from jax import lax
from jax.experimental import pallas as pl
from jax.experimental.pallas import tpu as pltpu
from jax.sharding import PartitionSpec as P

EPSILON = 1e-6
GELU_A = 0.7978845608028654
GELU_B = 0.7978845608028654 * 0.044715
CHUNK = 512
F_BLK = 256
FWD_SPLIT = 8
N_BLK = 256
VMEM_LIMIT = 67_043_328
LAGS = (3, 1, 2)
BF16 = jnp.bfloat16
F32 = jnp.float32


def dot(a, b):
    return jnp.dot(a, b, preferred_element_type=F32)


def dot_rt(a, b):
    return lax.dot_general(a, b, (((1,), (1,)), ((), ())), preferred_element_type=F32)


def inverse_rms(x_f32):
    return lax.rsqrt(jnp.mean(x_f32 * x_f32, axis=-1, keepdims=True) + EPSILON)


def gelu_of(a):
    t = jnp.tanh(a * (GELU_A + GELU_B * (a * a)))
    h = 0.5 * a
    return h + h * t


def gelu_and_slope(a):
    a2 = a * a
    t = jnp.tanh(a * (GELU_A + GELU_B * a2))
    h = 0.5 * a
    slope = (0.5 + 0.5 * t) + h * (1.0 - t * t) * (GELU_A + (3.0 * GELU_B) * a2)
    return h + h * t, slope


def fold_rows(v):
    return jnp.sum(v.reshape(v.shape[0] // 8, 8, v.shape[1]), axis=0)


def enter(stage, stages):
    barrier = pltpu.get_barrier_semaphore()
    for step in (1, stages - 1):
        pl.semaphore_signal(barrier, inc=1, device_id={"stage": lax.rem(stage + step, stages)},
                            device_id_type=pl.DeviceIdType.MESH)
    pl.semaphore_wait(barrier, 2)


def train_kernel(stages, seed_scale, lags, tokens, targets, w_in, w_out, gains, land, grad_in, grad_out_t,
                 grad_gain, sse, wi, wo_first, wo_ring, acc_in, acc_out, xs, dhs, outs, normed, normed_t, dh_t, sums,
                 hidden, da, w_sem, ring_sem, x_sem, dh_sem, flush_sem, send, recv):
    stage = lax.axis_index("stage")
    last = stages - 1
    count, _, d_model = tokens.shape
    d_ff = wi.shape[2]
    blocks = d_ff // F_BLK
    up_gap, back_gap, home_gap = lags
    lag_1 = (last - stage) * up_gap + 1
    lag_2 = last * up_gap + 2 + stage * back_gap
    lag_3 = last * (up_gap + back_gap) + 3 + (last - stage) * home_gap
    most_lag = last * (up_gap + back_gap + home_gap) + 3
    loads = [pltpu.make_async_copy(w_in, wi, w_sem.at[0]),
             pltpu.make_async_copy(w_out.at[0, pl.ds(0, F_BLK)], wo_first.at[0], w_sem.at[1]),
             pltpu.make_async_copy(w_out.at[1, pl.ds(0, F_BLK)], wo_first.at[1], w_sem.at[2])]
    for load in loads:
        load.start()
    grad_gain[...] = jnp.zeros_like(grad_gain)
    sse[...] = jnp.zeros_like(sse)
    enter(stage, stages)

    def place(k):
        q = lax.rem(k + 4, 4)
        tick = lax.div(k + 4, 4) - 1
        lag = jnp.where(q == 0, 0, jnp.where(q == 1, lag_1, jnp.where(q == 2, lag_2, lag_3)))
        c = tick - lag
        return q, c, (c >= 0) & (c < count)

    def row_of(q):
        return jnp.where((q == 0) | (q == 3), 0, 1)

    def hop(q, c):
        return pltpu.make_async_remote_copy(
            src_ref=outs.at[lax.rem(q, 2)], dst_ref=land.at[q, c], send_sem=send.at[q], recv_sem=recv.at[q, c],
            device_id={"stage": stage + 1 - 2 * lax.rem(q, 2)}, device_id_type=pl.DeviceIdType.MESH)

    def turn(q, c):
        return pltpu.make_async_copy(outs.at[lax.rem(q, 2)], land.at[q + 1, c], recv.at[q + 1, c])

    def leaves(q):
        p = lax.rem(q, 2)
        return ((p == 0) & (stage < last)) | ((p == 1) & (stage > 0))

    def turns(q):
        return ((lax.rem(q, 2) == 0) & (stage == last)) | ((q == 1) & (stage == 0))

    def from_turn(q):
        return ((lax.rem(q, 2) == 1) & (stage == last)) | ((q == 2) & (stage == 0))

    def arrived(q, c):
        pltpu.make_async_copy(outs.at[lax.rem(q, 2)], land.at[q, c], recv.at[q, c]).wait()

    def x_load(q, c):
        return pltpu.make_async_copy(land.at[row_of(q), c], xs.at[lax.rem(q, 2)], x_sem.at[lax.rem(q, 2)])

    def dh_load(q, c):
        return pltpu.make_async_copy(land.at[q, c], dhs.at[lax.rem(q, 2)], dh_sem.at[lax.rem(q, 2)])

    def issue(q, c):
        from_tokens = (row_of(q) == 0) & (stage == 0)

        @pl.when(from_tokens)
        def _():
            pltpu.make_async_copy(tokens.at[c], xs.at[lax.rem(q, 2)], x_sem.at[lax.rem(q, 2)]).start()

        @pl.when(jnp.logical_not(from_tokens))
        def _():
            x_load(q, c).start()

        @pl.when(q >= 2)
        def _():
            dh_load(q, c).start()

        @pl.when((q == 1) & (stage == 0))
        def _():
            pltpu.make_async_copy(targets.at[c], dhs.at[1], dh_sem.at[1]).start()

    def ring_load(row, block):
        return pltpu.make_async_copy(w_out.at[row, pl.ds(block * F_BLK, F_BLK)], wo_ring.at[block % 3],
                                     ring_sem.at[block % 3])

    def w_out_block(row, block):
        return wo_ring[block % 3] if block else wo_first[row]

    def columns(block):
        return slice(block * F_BLK, (block + 1) * F_BLK)

    def project(row, block):
        part = dot(hidden[block % 2], w_out_block(row, block))
        if block:
            sums[...] += part
        else:
            sums[...] = part

    def forward_block(row, block):
        if block >= 2:
            ring_load(row, block - 1).wait()
        if block + 1 < blocks:
            ring_load(row, block + 1).start()
        a = dot(normed[...], wi[row, :, columns(block)])
        if block:
            project(row, block - 1)
        hidden[block % 2] = gelu_of(a).astype(BF16)

    def forward_first(q, c):
        row = row_of(q)
        x_load(q, c).wait()
        x = xs[lax.rem(q, 2)].astype(F32)
        normed[...] = (x * inverse_rms(x) * gains[row]).astype(BF16)
        for block in range(FWD_SPLIT):
            forward_block(row, block)

    def forward_second(q, c):
        row = row_of(q)
        for block in range(FWD_SPLIT, blocks):
            forward_block(row, block)
        ring_load(row, blocks - 1).wait()
        out = sums[...] + dot(hidden[(blocks - 1) % 2], w_out_block(row, blocks - 1))
        outs[lax.rem(q, 2)] = (xs[lax.rem(q, 2)].astype(F32) + out).astype(BF16)

        @pl.when((q == 1) & (stage == 0))
        def _():
            dh_load(q, c).wait()
            error = outs[1].astype(F32) - dhs[1].astype(F32)
            sse[...] += fold_rows(error * error)
            outs[1] = (error * seed_scale).astype(BF16)

    def weight_grads(row, block):
        cols = columns(block)
        acc_out[row, :, cols] += dot(dh_t[...], hidden[block % 2])
        acc_in[row, :, cols] += dot(normed_t[...], da[:, cols])

    def clear():
        def piece(i, carry):
            rows = pl.ds(pl.multiple_of(i * 8, 8), 8)
            for row in range(2):
                acc_in[row, rows, :] = jnp.zeros((8, d_ff), F32)
                acc_out[row, rows, :] = jnp.zeros((8, d_ff), F32)
            return carry
        lax.fori_loop(0, d_model // 8, piece, 0)

    def backward_first(q, c):
        row = row_of(q)
        slot = lax.rem(q, 2)
        ring_load(row, 1).start()
        ring_load(row, 2).start()

        dh_load(q, c).wait()
        x_load(q, c).wait()
        x = xs[slot].astype(F32)
        n = (x * inverse_rms(x) * gains[row]).astype(BF16)
        normed[...] = n
        normed_t[...] = n.T
        dh_t[...] = dhs[slot].T
        for block in range(blocks):
            if block:
                ring_load(row, block).wait()
                if block + 2 < blocks:
                    ring_load(row, block + 2).start()
            du = dot_rt(dhs[slot], w_out_block(row, block))
            a = dot(normed[...], wi[row, :, columns(block)])
            if block:
                weight_grads(row, block - 1)
            u, slope = gelu_and_slope(a)
            hidden[block % 2] = u.astype(BF16)
            da[:, columns(block)] = (du * slope).astype(BF16)

    def backward_second(q, c):
        row = row_of(q)
        slot = lax.rem(q, 2)
        for n in range(0, d_model, N_BLK):
            sums[:, n:n + N_BLK] = dot_rt(da[...], wi[row, n:n + N_BLK, :])
        weight_grads(row, blocks - 1)
        x = xs[slot].astype(F32)
        inv = inverse_rms(x)
        grad_n = sums[...]
        xr = x * inv
        grad_gain[row] += fold_rows(xr * grad_n)
        scaled = grad_n * gains[row]
        mean = jnp.mean(xr * scaled, axis=-1, keepdims=True)
        outs[slot] = (dhs[slot].astype(F32) + inv * (scaled - xr * mean)).astype(BF16)

    def flushes(row):
        return [pltpu.make_async_copy(acc_in.at[row], grad_in.at[row], flush_sem.at[0, row]),
                pltpu.make_async_copy(acc_out.at[row], grad_out_t.at[row], flush_sem.at[1, row])]

    def step(k, carry):
        q, c, valid = place(k)
        q_next, c_next, valid_next = place(k + 1)

        @pl.when(valid & (q < 2))
        def _():
            forward_first(q, c)

        @pl.when(valid & (q >= 2))
        def _():
            backward_first(q, c)

        q_prev, c_prev, valid_prev = place(k - 1)

        @pl.when(valid_prev & turns(q_prev))
        def _():
            turn(q_prev, c_prev).wait()

        @pl.when(valid_next)
        def _():
            @pl.when(((q_next > 0) | (stage > 0)) & jnp.logical_not(from_turn(q_next)))
            def _():
                arrived(q_next, c_next)
            issue(q_next, c_next)

        @pl.when((k == 1) & (stage == 0))
        def _():
            clear()

        @pl.when(k == 4 * (count + lag_2))
        def _():
            for flush in flushes(1):
                flush.start()

        q_slot, c_slot, used_slot = place(k - 2)

        @pl.when(valid & used_slot & leaves(q))
        def _():
            hop(q_slot, c_slot).wait_send()

        @pl.when(valid & jnp.logical_not(used_slot) & (c >= 1) & leaves(q))
        def _():
            hop(q, c - 1).wait_send()

        @pl.when(valid & (q < 2))
        def _():
            forward_second(q, c)

        @pl.when(valid & (q >= 2))
        def _():
            backward_second(q, c)

        @pl.when(valid & leaves(q))
        def _():
            hop(q, c).start()

        @pl.when(valid & turns(q))
        def _():
            turn(q, c).start()
        return carry

    @pl.when(stage > 0)
    def _():
        clear()
    for load in loads:
        load.wait()

    @pl.when(stage > 0)
    def _():
        arrived(0, 0)
    issue(0, 0)
    lax.fori_loop(0, 4 * (count + most_lag), step, 0)
    for flush in flushes(0):
        flush.start()
    for q in (2, 3):
        @pl.when(leaves(q))
        def _(q=q):
            hop(q, count - 1).wait_send()
    for row in (1, 0):
        for flush in flushes(row):
            flush.wait()


def solution(mesh):
    stages = mesh.shape['stage']

    def device_step(tokens, targets, w_in, w_out, norm_gains):
        micro_count, tokens_mb, d_model = tokens.shape
        d_ff = w_in.shape[2]
        total = micro_count * tokens_mb
        count = total // CHUNK
        tokens = tokens.reshape(count, CHUNK, d_model)
        targets = targets.reshape(count, CHUNK, d_model)
        gains = norm_gains.reshape(2, 1, d_model)
        any_spec = pl.BlockSpec(memory_space=pl.ANY)
        vmem_spec = pl.BlockSpec(memory_space=pltpu.VMEM)
        dma = pltpu.SemaphoreType.DMA
        flops = 7 * 2 * 2 * total * d_model * d_ff
        grad_shape = jax.ShapeDtypeStruct((2, d_model, d_ff), F32)

        _, grad_in, grad_out_t, grad_gain, sse = pl.pallas_call(
            functools.partial(train_kernel, stages, 2.0 / total, LAGS),
            out_shape=(jax.ShapeDtypeStruct((4, count, CHUNK, d_model), BF16), grad_shape, grad_shape,
                       jax.ShapeDtypeStruct((2, 8, d_model), F32), jax.ShapeDtypeStruct((8, d_model), F32)),
            in_specs=[any_spec] * 4 + [vmem_spec],
            out_specs=(any_spec, any_spec, any_spec, vmem_spec, vmem_spec),
            scratch_shapes=[
                pltpu.VMEM((2, d_model, d_ff), BF16),
                pltpu.VMEM((2, F_BLK, d_model), BF16), pltpu.VMEM((3, F_BLK, d_model), BF16),
                pltpu.VMEM((2, d_model, d_ff), F32), pltpu.VMEM((2, d_model, d_ff), F32),
                pltpu.VMEM((2, CHUNK, d_model), BF16), pltpu.VMEM((2, CHUNK, d_model), BF16),
                pltpu.VMEM((2, CHUNK, d_model), BF16),
                pltpu.VMEM((CHUNK, d_model), BF16),
                pltpu.VMEM((d_model, CHUNK), BF16), pltpu.VMEM((d_model, CHUNK), BF16),
                pltpu.VMEM((CHUNK, d_model), F32),
                pltpu.VMEM((2, CHUNK, F_BLK), BF16), pltpu.VMEM((CHUNK, d_ff), BF16),
                dma((3,)), dma((3,)), dma((2,)), dma((2,)), dma((2, 2)), dma((4,)), dma((4, count)),
            ],
            compiler_params=pltpu.CompilerParams(collective_id=0, has_side_effects=True,
                                                 vmem_limit_bytes=VMEM_LIMIT),
            cost_estimate=pl.CostEstimate(flops=flops, bytes_accessed=10 ** 8, transcendentals=0),
        )(tokens, targets, w_in, w_out, gains)

        loss_value = lax.psum(jnp.sum(sse), 'stage') / (total * d_model)
        return grad_in, jnp.swapaxes(grad_out_t, 1, 2), jnp.sum(grad_gain, axis=1), loss_value.reshape(1)

    block_spec = P(('dp', 'stage'))
    return jax.shard_map(device_step, mesh=mesh,
                         in_specs=(P('dp'), P('dp'), P('stage'), P('stage'), P('stage')),
                         out_specs=(block_spec, block_spec, block_spec, P('dp')),
                         check_vma=False)
```

time: 4440 us -> 1880 us (0.42)
  matrix products: 2390 us -> 0 us
  Pallas kernels: 0 us -> 1780 us
  waiting for transfers between devices: 649 us -> 0 us
  other arithmetic: 509 us -> 1.97 us
  starting transfers between devices: 486 us -> 0 us
  local copies, waits for them, and re-layouts: 231 us -> 32.9 us
  loops' own time: 147 us -> 0 us
  blocking collectives: 6.27 us -> 52 us
    dot_general x192 -> x0, matrix products: 2390 us -> none  [the longest x32 487 us: layer_forward(): out_f32 = jnp.dot(hidden, second_w, preferred_element_type=jnp.float32)]
    pallas_call x0 -> x1, Pallas kernels: none -> 1780 us  [device_step(): pl.pallas_call(functools.partial(train_kernel, stages, 2.0 / total, LAGS)...]
    ppermute x92 -> x0, waiting for transfers between devices: 649 us -> none  [the longest x23 383 us: backward_tick(): recv_up = lax.ppermute(grad_up_out, 'stage', down_perm)]
    ppermute x92 -> x0, starting transfers between devices: 486 us -> none  [the longest x23 173 us: backward_tick(): recv_up = lax.ppermute(grad_up_out, 'stage', down_perm)]
    select_n x85 -> x0, other arithmetic: 174 us -> none  [the longest x23 63.3 us: backward_tick(): next_down = jnp.where(is_last, grad_up_out, recv_down)]
    another operation x94 -> x0, loops' own time: 147 us -> none  [the longest x1 41.9 us: device_step(): back_state, _ = lax.scan(backward_tick, back_init, jnp.arange(tick_count))]
    dynamic_slice x115 -> x0, local copies, waits for them, and re-layouts: 133 us -> none  [the longest x46 69.8 us: store_inputs(): old_rows = lax.dynamic_index_in_dim(buffer_all, mb_index, 1, keepdims=False)]
    reduce_sum x65 -> x2, other arithmetic: 100 us -> 1.97 us  [the longest x1 1.35 us: device_step(): loss_value = lax.psum(jnp.sum(sse), 'stage') / (total * d_model)]
  transfers between devices with their start and end apart: 92 -> 0, of which waited for: 57 -> 0; matrix products, arithmetic and copies ran while one was open for 37% -> 0% of each run, Pallas kernels for 0% -> 0%
where the time goes in v2:
time: 1880 us; the launch traced here: 1870 us
  Pallas kernels  1780 us (95%)
  blocking collectives  52 us (3%)
  local copies, waits for them, and re-layouts  32.9 us (2%)
    pallas_call x1, Pallas kernels, device_step(): pl.pallas_call(functools.partial(train_kernel, stages, 2.0 / total, LAGS)...  1780 us
    psum x1, blocking collectives, device_step(): loss_value = lax.psum(jnp.sum(sse), 'stage') / (total * d_model)  52 us

profile of v2, /device:TPU:6, one launch (start us, length us, event | category | flops | bytes accessed | tf_op | source)
XLA Modules:
  0.0 1872.8 jit_solution(13236948102451079565)
XLA Ops:
  0.6 1.3 reshape.22.gains
  1.9 1783.6 %shard_map.84 = (bf16[4,32,512,768]{3,2,1,0:T(8,128)(2,1)}, f32[2,768,3072]{2,1,0:T(8,128)}, f32[2,768,3072]{2,1,0:T(8,128)}, f32[2,8,768]{2,1,0:T(8,128)}, f32[8,768]{1,0:T(8,128)}) custom-call(bf16[32,512,768]{2,1,0:T(8,128)(2,1)} %bitcast.5, bf16[32,512,768]{2,1,0:T(8,128)(2,1)} %bitcast.6, bf16[2,768,3072]{2,1,0:T(8,128)(2,1)} %w_in.1, ...), custom_call_target="tpu_custom_call" | custom-call | flops 1082331758592 | bytes 100000000 | tf_op jit(solution)/shard_map/pallas_call | solution.py:348
  1785.5 1.3 reduce_sum.19
  1786.8 52.0 %psum.7 = f32[]{:T(128)} all-reduce(f32[]{:T(128)} %reduce_sum.19), channel_id=1, replica_groups=mesh['dp'=2,'stage'=4] {'stage'}, use_global_device_ids=true, to_apply=%region_2.0 | all-reduce | flops 1 | bytes 8 | tf_op jit(solution)/shard_map/psum | solution.py:371
  1839.5 0.0 copy-start
  1839.5 18.7 copy.9
  1858.2 0.0 copy-done
  1858.2 0.6 reduce_sum.18
  1858.8 12.9 copy.11
Async XLA Ops:
  1839.5 18.7 copy-start
